TPU v7x, 128 devices: a whole 4x4x4 slice. The times are simulated.
128 devices in a mesh: dp: 8 (over y, core), pipe: 4 (over x), tensor: 4 (over z).
Axes of the slice: x: 4, y: 4, z: 4, core: 2. Of those that a mesh axis runs over, the one named last changes fastest.
Arguments:
- query_states: bfloat16 [16, 512, 1024], P('dp'), may hold values from -6 to 6
- doc_states: bfloat16 [16, 512, 1024], P('dp'), may hold values from -6 to 6
- query_len: int32 [16], P('dp'), may hold values from 64 to 512
- doc_len: int32 [16], P('dp'), may hold values from 64 to 512
- doc_order: int32 [8, 2], P('dp'), may hold values from 0 to 1, each once within a row
- w_qkv: bfloat16 [4, 3, 1024, 1024], P('pipe', None, None, 'tensor'), may hold values from -0.1875 to 0.1875
- w_out: bfloat16 [4, 1024, 1024], P('pipe', 'tensor'), may hold values from -0.1875 to 0.1875
- w_up: bfloat16 [4, 1024, 4096], P('pipe', None, 'tensor'), may hold values from -0.1875 to 0.1875
- w_down: bfloat16 [4, 4096, 1024], P('pipe', 'tensor'), may hold values from -0.09375 to 0.09375
- gain_attn: float32 [4, 1024], P('pipe'), may hold values from 0.1 to 1.9
- gain_mlp: float32 [4, 1024], P('pipe'), may hold values from 0.1 to 1.9
Outputs:
- query_vectors: bfloat16 [16, 1024], P('dp', ('pipe', 'tensor'))
- document_vectors: bfloat16 [16, 1024], P('dp', ('pipe', 'tensor'))
- pair_loss: float32 [16], P('dp')
Inputs may be any that keep to these rules, and one draw needn't show every extreme that they name: `doc_order`: each row holds every number of 0 to 1 once.
All inputs are finite; a program needn't handle non-finite values.
Results may differ from a plain program's by a relative error of at most 0.035.
Values may be sent and summed in bfloat16 or wider, within the bound.
A program may use at most 192 MiB of HBM per device.

v0:
```python
import math
import jax
import jax.numpy as jnp
from jax import lax
from jax.sharding import PartitionSpec as P

D = 1024
HEADS = 16
SOFTMAX_TEMPER = 0.05
EPSILON = 1e-06
LAYER_EPSILON = 1e-12


def from_behind(value, axis, steps):
    count = lax.axis_size(axis)
    initial, last = (max(0, -steps), min(count, count - steps))
    return lax.ppermute(value, axis, [(source, source + steps) for source in range(initial, last)])


def from_root(x, axis, root):
    return lax.dynamic_index_in_dim(lax.all_gather(x, axis), root, 0, keepdims=False)


def laid_out(parts, dim):
    lengths = list(parts.shape[1:])
    lengths[dim] *= parts.shape[0]
    return jnp.moveaxis(parts, 0, dim).reshape(lengths)


def copy_for_each(x, axis):
    peers = lax.axis_size(axis)
    return lax.all_to_all(jnp.broadcast_to(x[None], (peers, *x.shape)), axis, 0, 0, tiled=True)


def collect(x, axis, dim):
    return laid_out(copy_for_each(x, axis), dim)


def of_everyone(x, axis):
    return copy_for_each(x, axis).sum(axis=0)


def norm_rows(values_in, gain_row):
    row_mean = jnp.mean(values_in, axis=-1, keepdims=True)
    centered = values_in - row_mean
    variance = jnp.mean(centered * centered, axis=-1, keepdims=True)
    return centered * lax.rsqrt(variance + LAYER_EPSILON) * gain_row


def local_reduce(left_side, right_side, residual, gain_row, group_count):
    row_total = left_side.shape[0]
    group_width = left_side.shape[1] // group_count
    left_parts = left_side.reshape(row_total, group_count, group_width)
    right_parts = right_side.reshape(group_count, group_width, right_side.shape[1])
    partials = jnp.einsum(
        "sgk,gkd->gsd", left_parts, right_parts, preferred_element_type=jnp.float32
    )
    summed = jnp.sum(partials.astype(jnp.bfloat16).astype(jnp.float32), axis=0)
    return norm_rows(residual.astype(jnp.float32) + summed, gain_row).astype(jnp.bfloat16)


def reduce_block(left_side, right_side, residual, gain_row, group_count):
    return local_reduce(left_side, right_side, residual, gain_row, group_count)


def encode_layer(hidden, valid_keys, w_qkv, w_out, w_up, w_down, gain_attn, gain_mlp, group_count):
    head_width = D // HEADS
    local_width = w_qkv.shape[-1]
    head_count = local_width // head_width
    slot_count = hidden.shape[0]
    inv_sqrt = 1.0 / math.sqrt(head_width)
    query_rows = (jnp.dot(hidden, w_qkv[0], preferred_element_type=jnp.float32) * inv_sqrt).astype(
        jnp.bfloat16
    )
    key_rows = jnp.dot(hidden, w_qkv[1], preferred_element_type=jnp.float32).astype(jnp.bfloat16)
    value_rows = jnp.dot(hidden, w_qkv[2], preferred_element_type=jnp.float32).astype(jnp.bfloat16)
    query_heads = query_rows.reshape(slot_count, head_count, head_width)
    key_heads = key_rows.reshape(slot_count, head_count, head_width)
    value_heads = value_rows.reshape(slot_count, head_count, head_width)
    scores = jnp.einsum("qhe,khe->hqk", query_heads, key_heads, preferred_element_type=jnp.float32)
    exp_scores = jnp.where(valid_keys[None, None, :], jnp.exp(scores), 0.0)
    attention = (exp_scores / jnp.sum(exp_scores, axis=-1, keepdims=True)).astype(jnp.bfloat16)
    context = jnp.einsum("hqk,khe->qhe", attention, value_heads, preferred_element_type=jnp.float32)
    context = context.astype(jnp.bfloat16).reshape(slot_count, local_width)
    mixed = reduce_block(context, w_out, hidden, gain_attn, group_count)
    upward = jnp.dot(mixed, w_up, preferred_element_type=jnp.float32)
    activated = jax.nn.gelu(upward, approximate=False).astype(jnp.bfloat16)
    return reduce_block(activated, w_down, mixed, gain_mlp, group_count)


def interior_rows(left_side, right_side):
    return lax.dot_general(
        left_side, right_side, (((1,), (1,)), ((), ())), preferred_element_type=jnp.float32
    )


def per_device(
    query_states,
    doc_states,
    query_len,
    doc_len,
    doc_order,
    w_qkv,
    w_out,
    w_up,
    w_down,
    gain_attn,
    gain_mlp,
):
    pair_count = query_states.shape[0]
    seq_count = 2 * pair_count
    slot_count = query_states.shape[1]
    model_width = query_states.shape[2]
    section_count = lax.axis_size("pipe")
    section_index = lax.axis_index("pipe")
    tensor_count = lax.axis_size("tensor")
    lengths = jnp.concatenate([query_len, doc_len])
    positions = jnp.arange(slot_count, dtype=jnp.int32)
    piece_width = model_width // (section_count * tensor_count)
    w_qkv, w_out, w_up, w_down = (
        lax.all_gather(w_qkv, "tensor", axis=3, tiled=True),
        lax.all_gather(w_out, "tensor", axis=1, tiled=True),
        lax.all_gather(w_up, "tensor", axis=2, tiled=True),
        lax.all_gather(w_down, "tensor", axis=1, tiled=True),
    )
    share = seq_count // tensor_count
    first_seq = lax.axis_index("tensor") * share
    local_ids = jnp.arange(share, dtype=jnp.int32)

    def tick_step(tick_index, state_pair):
        passed, pooled = state_pair
        entry_index = first_seq + jnp.clip(tick_index, 0, share - 1)
        query_pick = query_states[jnp.minimum(entry_index, pair_count - 1)]
        doc_pick = doc_states[jnp.clip(entry_index - pair_count, 0, pair_count - 1)]
        fresh = jnp.where(entry_index < pair_count, query_pick, doc_pick)
        hidden = jnp.where(section_index == 0, fresh, passed)
        local_index = jnp.clip(tick_index - section_index, 0, share - 1)
        seq_length = lengths[first_seq + local_index]
        valid_keys = positions < seq_length
        hidden = encode_layer(
            hidden,
            valid_keys,
            w_qkv[0],
            w_out[0],
            w_up[0],
            w_down[0],
            gain_attn[0],
            gain_mlp[0],
            tensor_count,
        )
        finished = tick_index - (section_count - 1)
        store_now = (section_index == section_count - 1) & (finished >= 0)
        summed = jnp.sum(jnp.where(valid_keys[:, None], hidden.astype(jnp.float32), 0.0), axis=0)
        mean_row = summed / seq_length.astype(jnp.float32)
        row_mask = (local_ids == local_index) & store_now
        pooled = jnp.where(row_mask[:, None], mean_row[None, :], pooled)
        passed = from_behind(hidden, "pipe", 1)
        return (passed, pooled)

    start_pair = (
        jnp.zeros((slot_count, model_width), jnp.bfloat16),
        jnp.zeros((share, model_width), jnp.float32),
    )
    unused_state, pooled = lax.fori_loop(0, share + section_count - 1, tick_step, start_pair)
    embedded = (
        pooled * lax.rsqrt(jnp.sum(pooled * pooled, axis=1, keepdims=True) + EPSILON)
    ).astype(jnp.bfloat16)
    grouped = embedded.reshape(share, section_count, tensor_count, piece_width)
    moved = lax.all_to_all(grouped, "tensor", split_axis=2, concat_axis=0, tiled=True)
    tensor_cols = moved.reshape(seq_count, section_count, piece_width)
    shared = from_root(tensor_cols, "pipe", section_count - 1)
    own_piece = lax.dynamic_index_in_dim(shared, section_index, 1, keepdims=False)
    query_portion = own_piece[:pair_count]
    document_portion = own_piece[pair_count:]
    order_row = doc_order[0]
    data_count = lax.axis_size("dp")
    partial_table = interior_rows(query_portion, collect(document_portion, "dp", 0))
    score_table = of_everyone(partial_table, ("pipe", "tensor")) / SOFTMAX_TEMPER
    column_ids = jnp.arange(pair_count * data_count, dtype=jnp.int32)
    target = lax.axis_index("dp") * pair_count + order_row
    is_positive = column_ids[None, :] == target[:, None]
    positive_score = jnp.sum(jnp.where(is_positive, score_table, 0.0), axis=1)
    exp_total = jnp.sum(jnp.exp(score_table), axis=1)
    pair_loss = jnp.log(exp_total) - positive_score
    return (query_portion, document_portion, pair_loss)


def solution(mesh):
    in_specs = (
        P("dp", None, None),
        P("dp", None, None),
        P("dp"),
        P("dp"),
        P("dp", None),
        P("pipe", None, None, "tensor"),
        P("pipe", "tensor", None),
        P("pipe", None, "tensor"),
        P("pipe", "tensor", None),
        P("pipe", None),
        P("pipe", None),
    )
    out_specs = (P("dp", ("pipe", "tensor")), P("dp", ("pipe", "tensor")), P("dp"))
    return jax.shard_map(
        per_device, mesh=mesh, in_specs=in_specs, out_specs=out_specs, check_vma=False
    )
```

profile of v0, /device:TPU:0, one launch (start us, length us, event | category | flops | bytes accessed | tf_op | source)
XLA Modules:
  0.0 658.8 jit_solution(12119853464796553148)
XLA Ops:
  10.7 32.4 %all-gather.8.cloned.1.call-done = bf16[1,1024,1024]{2,1,0:T(8,128)(2,1)} async-done(((bf16[1,256,1024]{2,1,0:T(8,128)(2,1)}), bf16[1,1024,1024]{2,1,0:T(8,128)(2,1)}) %all-gather.8.cloned.1.call-update) | async-done | bytes 2097168 | tf_op jit(solution)/shard_map/all_gather | solution.py:122
  43.2 70.9 %all-gather.6.cloned.1.call-done = bf16[1,3,1024,1024]{3,2,1,0:T(8,128)(2,1)} async-done(((bf16[1,3,1024,256]{3,2,1,0:T(8,128)(2,1)}), bf16[1,3,1024,1024]{3,2,1,0:T(8,128)(2,1)}) %all-gather.6.cloned.1.call-update) | async-done | bytes 6291472 | tf_op jit(solution)/shard_map/all_gather | solution.py:121
  114.0 85.5 %all-gather.10.cloned.1.call-done = bf16[1,1024,4096]{2,1,0:T(8,128)(2,1)} async-done(((bf16[1,1024,1024]{2,1,0:T(8,128)(2,1)}), bf16[1,1024,4096]{2,1,0:T(8,128)(2,1)}) %all-gather.10.cloned.1.call-update) | async-done | bytes 8388624 | tf_op jit(solution)/shard_map/all_gather | solution.py:123
  199.5 85.6 %all-gather.12.cloned.1.call-done = bf16[1,4096,1024]{2,1,0:T(8,128)(2,1)} async-done(((bf16[1,1024,1024]{2,1,0:T(8,128)(2,1)}), bf16[1,4096,1024]{2,1,0:T(8,128)(2,1)}) %all-gather.12.cloned.1.call-update) | async-done | bytes 8388624 | tf_op jit(solution)/shard_map/all_gather | solution.py:124
  285.3 318.5 %while.18 = (s32[]{:T(128)}, bf16[512,1024]{1,0:T(8,128)(2,1)S(1)}, f32[1,1024]{1,0:T(1,128)S(1)}, pred[]{:T(512)}, s32[]{:T(128)}, /*index=5*/bf16[2,512,1024]{...) while((s32[]{:T(128)}, bf16[512,1024]{1,0:T(8,128)(2,1)S(1)}, ...), condition=%wide.region_9.10_spmd.clone, body=%wide.region_0.9_spmd.clone.sunk | while | flops 14147382272 | bytes 201497376 | solution.py:164
  285.3 1.8 bitcast_select_fusion.2
  287.2 3.0 multiply_convert_fusion.6
  290.2 2.2 fusion.92
  292.4 2.3 fusion.91
  295.3 1.5 copy.80
  298.1 2.3 copy.78
  300.3 3.8 fusion.93
  304.1 3.1 fusion.94
  307.3 1.3 convert_reduce_fusion.5
  311.0 22.6 %fusion.96 = bf16[512,4096]{1,0:T(8,128)(2,1)S(1)} fusion(bf16[512,1024]{1,0:T(8,128)(2,1)S(1)} %multiply_convert_fusion.7, bf16[1,1024,4096]{2,1,0:T(8,128)(2,1)S(1)} %bitcast.137), kind=kOutput, calls=%fused_computation.7.clone.1 | convolution fusion | flops 4431282176 | bytes 13631488 | tf_op jit(solution)/shard_map/while/body/eval_jaxpr/dot_general | solution.py:86
  333.7 4.9 convert_reduce_fusion.6
  339.9 3.4 collective-permute-start
  344.0 21.5 %collective-permute-done = bf16[512,1024]{1,0:T(8,128)(2,1)S(1)} collective-permute-done((bf16[512,1024]{1,0:T(8,128)(2,1)S(1)}, bf16[512,1024]{1,0:T(8,128)(2,1)S(1)}, u32[]{:S(2)}, u32[]{:S(2)}) %collective-permute-start) | collective-permute-done | bytes 1048608 | tf_op jit(solution)/shard_map/while/body/eval_jaxpr/ppermute | solution.py:17
  365.5 1.8 bitcast_select_fusion.2
  367.3 3.0 multiply_convert_fusion.6
  370.4 2.2 fusion.92
  372.6 2.3 fusion.91
  375.5 1.5 copy.80
  378.2 2.3 copy.78
  380.5 3.8 fusion.93
  384.3 3.1 fusion.94
  387.5 1.3 convert_reduce_fusion.5
  391.2 22.6 %fusion.96 = bf16[512,4096]{1,0:T(8,128)(2,1)S(1)} fusion(bf16[512,1024]{1,0:T(8,128)(2,1)S(1)} %multiply_convert_fusion.7, bf16[1,1024,4096]{2,1,0:T(8,128)(2,1)S(1)} %bitcast.137), kind=kOutput, calls=%fused_computation.7.clone.1 | convolution fusion | flops 4431282176 | bytes 13631488 | tf_op jit(solution)/shard_map/while/body/eval_jaxpr/dot_general | solution.py:86
  413.8 4.9 convert_reduce_fusion.6
  420.0 4.4 collective-permute-start
  425.2 20.6 %collective-permute-done = bf16[512,1024]{1,0:T(8,128)(2,1)S(1)} collective-permute-done((bf16[512,1024]{1,0:T(8,128)(2,1)S(1)}, bf16[512,1024]{1,0:T(8,128)(2,1)S(1)}, u32[]{:S(2)}, u32[]{:S(2)}) %collective-permute-start) | collective-permute-done | bytes 1048608 | tf_op jit(solution)/shard_map/while/body/eval_jaxpr/ppermute | solution.py:17
  445.8 1.8 bitcast_select_fusion.2
  447.6 3.0 multiply_convert_fusion.6
  450.7 2.2 fusion.92
  452.9 2.3 fusion.91
  455.8 1.5 copy.80
  458.5 2.3 copy.78
  460.8 3.8 fusion.93
  464.6 3.1 fusion.94
  467.8 1.3 convert_reduce_fusion.5
  471.5 22.6 %fusion.96 = bf16[512,4096]{1,0:T(8,128)(2,1)S(1)} fusion(bf16[512,1024]{1,0:T(8,128)(2,1)S(1)} %multiply_convert_fusion.7, bf16[1,1024,4096]{2,1,0:T(8,128)(2,1)S(1)} %bitcast.137), kind=kOutput, calls=%fused_computation.7.clone.1 | convolution fusion | flops 4431282176 | bytes 13631488 | tf_op jit(solution)/shard_map/while/body/eval_jaxpr/dot_general | solution.py:86
  494.1 4.9 convert_reduce_fusion.6
  500.3 4.4 collective-permute-start
  505.4 19.8 %collective-permute-done = bf16[512,1024]{1,0:T(8,128)(2,1)S(1)} collective-permute-done((bf16[512,1024]{1,0:T(8,128)(2,1)S(1)}, bf16[512,1024]{1,0:T(8,128)(2,1)S(1)}, u32[]{:S(2)}, u32[]{:S(2)}) %collective-permute-start) | collective-permute-done | bytes 1048608 | tf_op jit(solution)/shard_map/while/body/eval_jaxpr/ppermute | solution.py:17
  525.2 1.8 bitcast_select_fusion.2
  527.1 3.0 multiply_convert_fusion.6
  530.1 2.2 fusion.92
  532.3 2.3 fusion.91
  535.2 1.5 copy.80
  538.0 2.3 copy.78
  540.2 3.8 fusion.93
  544.0 3.1 fusion.94
  547.2 1.3 convert_reduce_fusion.5
  550.9 22.6 %fusion.96 = bf16[512,4096]{1,0:T(8,128)(2,1)S(1)} fusion(bf16[512,1024]{1,0:T(8,128)(2,1)S(1)} %multiply_convert_fusion.7, bf16[1,1024,4096]{2,1,0:T(8,128)(2,1)S(1)} %bitcast.137), kind=kOutput, calls=%fused_computation.7.clone.1 | convolution fusion | flops 4431282176 | bytes 13631488 | tf_op jit(solution)/shard_map/while/body/eval_jaxpr/dot_general | solution.py:86
  573.5 4.9 convert_reduce_fusion.6
  579.8 4.4 collective-permute-start
  584.9 18.9 %collective-permute-done = bf16[512,1024]{1,0:T(8,128)(2,1)S(1)} collective-permute-done((bf16[512,1024]{1,0:T(8,128)(2,1)S(1)}, bf16[512,1024]{1,0:T(8,128)(2,1)S(1)}, u32[]{:S(2)}, u32[]{:S(2)}) %collective-permute-start) | collective-permute-done | bytes 1048608 | tf_op jit(solution)/shard_map/while/body/eval_jaxpr/ppermute | solution.py:17
  605.9 4.0 all-to-all-start
  609.9 5.3 all-to-all-done
  615.2 13.3 %all-gather = bf16[16,1,4,1,64]{4,2,3,1,0:T(4,128)(2,1)S(1)} all-gather(bf16[4,1,4,1,64]{4,2,3,1,0:T(4,128)(2,1)S(1)} %bitcast_bitcast_fusion), channel_id=2, replica_groups=mesh['dp'=8,'pipe'=4,'tensor'=4] {'pipe'}, dimensions={0}, use_global_device_ids=true | all-gather | bytes 10240 | tf_op jit(solution)/shard_map/all_gather | solution.py:21
  629.2 4.3 all-to-all-start.1
  633.5 5.3 all-to-all-done.1
  639.5 4.4 all-to-all-start.2
  643.9 7.6 %all-to-all-done.2 = f32[16,2,16]{2,1,0:T(2,128)S(1)} async-done(((f32[16,2,16]{2,1,0:T(2,128)}), f32[16,2,16]{2,1,0:T(2,128)S(1)}, u32[]{:S(2)}, u32[]{:S(2)}) %all-to-all-start.2) | async-done | bytes 2080 | tf_op jit(solution)/shard_map/all_to_all | solution.py:32
  (187 shorter events, 29.2 us)
Async XLA Ops:
  7.2 36.0 %all-gather.8.cloned.1.call-start = ((), (), s32[]{:S(2)}) async-start(), calls=%async_computation.4 | async-start | bytes 2621440 | tf_op jit(solution)/shard_map/all_gather | solution.py:122
  7.9 106.1 %all-gather.6.cloned.1.call-start = ((), (), s32[]{:S(2)}) async-start(), calls=%async_computation.3 | async-start | bytes 7864320 | tf_op jit(solution)/shard_map/all_gather | solution.py:121
  8.6 190.9 %all-gather.10.cloned.1.call-start = ((), (), s32[]{:S(2)}) async-start(), calls=%async_computation.5 | async-start | bytes 10485760 | tf_op jit(solution)/shard_map/all_gather | solution.py:123
  9.4 275.8 %all-gather.12.cloned.1.call-start = ((), (), s32[]{:S(2)}) async-start(), calls=%async_computation.6 | async-start | bytes 10485760 | tf_op jit(solution)/shard_map/all_gather | solution.py:124
  285.3 358.6 %copy-start.6 = (s32[1,2]{1,0:T(1,128)S(1)}, s32[1,2]{1,0:T(1,128)}, u32[]{:S(2)}) copy-start(s32[1,2]{1,0:T(1,128)} %param.17) | copy-start | bytes 28
  285.3 4.9 slice-start.4
  287.2 3.0 slice-start.5
  300.3 3.8 copy-start
  304.1 3.2 copy-start.5
  307.3 2.2 copy-start.2
  307.3 2.6 slice-start
  308.6 2.4 slice-start.1
  309.0 24.7 %slice-start.2 = ((s8[8388608]{0:T(1024)(128)(4,1)}), s8[4194304]{0:T(1024)(128)(4,1)S(1)}, s32[]{:S(2)}) async-start(s8[8388608]{0:T(1024)(128)(4,1)} %bitcast.138), calls=%async_computation.9 | async-start | bytes 8388608 | tf_op jit(solution)/shard_map/while
  311.0 22.6 %slice-start.3 = ((s8[8388608]{0:T(1024)(128)(4,1)}), s8[4194304]{0:T(1024)(128)(4,1)S(1)}, s32[]{:S(2)}) async-start(s8[8388608]{0:T(1024)(128)(4,1)} %bitcast.138), calls=%async_computation.10 | async-start | bytes 8388608 | tf_op jit(solution)/shard_map/while
  333.6 5.7 copy-start.1
  339.9 25.6 %collective-permute-start = (bf16[512,1024]{1,0:T(8,128)(2,1)S(1)}, bf16[512,1024]{1,0:T(8,128)(2,1)S(1)}, u32[]{:S(2)}, u32[]{:S(2)}) collective-permute-start(bf16[512,1024]{1,0:T(8,128)(2,1)S(1)} %get-tuple-element.564), channel_id=1, source_target_pairs={{0,4},{4,8},{8,12},{1,5},{5,9},{9,13},{2,6},{6,10},{10,14},{3,7},{... | collective-permute-start | bytes 3145736 | tf_op jit(solution)/shard_map/while/body/eval_jaxpr/ppermute | solution.py:17
  365.5 4.8 slice-start.4
  367.3 3.0 slice-start.5
  380.5 3.8 copy-start
  384.3 3.2 copy-start.5
  387.4 2.2 copy-start.2
  387.4 2.6 slice-start
  388.8 2.4 slice-start.1
  389.1 24.7 %slice-start.2 = ((s8[8388608]{0:T(1024)(128)(4,1)}), s8[4194304]{0:T(1024)(128)(4,1)S(1)}, s32[]{:S(2)}) async-start(s8[8388608]{0:T(1024)(128)(4,1)} %bitcast.138), calls=%async_computation.9 | async-start | bytes 8388608 | tf_op jit(solution)/shard_map/while
  391.2 22.6 %slice-start.3 = ((s8[8388608]{0:T(1024)(128)(4,1)}), s8[4194304]{0:T(1024)(128)(4,1)S(1)}, s32[]{:S(2)}) async-start(s8[8388608]{0:T(1024)(128)(4,1)} %bitcast.138), calls=%async_computation.10 | async-start | bytes 8388608 | tf_op jit(solution)/shard_map/while
  413.8 5.7 copy-start.1
  420.0 25.8 %collective-permute-start = (bf16[512,1024]{1,0:T(8,128)(2,1)S(1)}, bf16[512,1024]{1,0:T(8,128)(2,1)S(1)}, u32[]{:S(2)}, u32[]{:S(2)}) collective-permute-start(bf16[512,1024]{1,0:T(8,128)(2,1)S(1)} %get-tuple-element.564), channel_id=1, source_target_pairs={{0,4},{4,8},{8,12},{1,5},{5,9},{9,13},{2,6},{6,10},{10,14},{3,7},{... | collective-permute-start | bytes 3145736 | tf_op jit(solution)/shard_map/while/body/eval_jaxpr/ppermute | solution.py:17
  445.8 4.8 slice-start.4
  447.6 3.0 slice-start.5
  460.8 3.8 copy-start
  464.6 3.2 copy-start.5
  467.7 2.2 copy-start.2
  467.7 2.6 slice-start
  469.1 2.4 slice-start.1
  469.4 24.7 %slice-start.2 = ((s8[8388608]{0:T(1024)(128)(4,1)}), s8[4194304]{0:T(1024)(128)(4,1)S(1)}, s32[]{:S(2)}) async-start(s8[8388608]{0:T(1024)(128)(4,1)} %bitcast.138), calls=%async_computation.9 | async-start | bytes 8388608 | tf_op jit(solution)/shard_map/while
  471.5 22.6 %slice-start.3 = ((s8[8388608]{0:T(1024)(128)(4,1)}), s8[4194304]{0:T(1024)(128)(4,1)S(1)}, s32[]{:S(2)}) async-start(s8[8388608]{0:T(1024)(128)(4,1)} %bitcast.138), calls=%async_computation.10 | async-start | bytes 8388608 | tf_op jit(solution)/shard_map/while
  494.1 5.7 copy-start.1
  500.3 24.9 %collective-permute-start = (bf16[512,1024]{1,0:T(8,128)(2,1)S(1)}, bf16[512,1024]{1,0:T(8,128)(2,1)S(1)}, u32[]{:S(2)}, u32[]{:S(2)}) collective-permute-start(bf16[512,1024]{1,0:T(8,128)(2,1)S(1)} %get-tuple-element.564), channel_id=1, source_target_pairs={{0,4},{4,8},{8,12},{1,5},{5,9},{9,13},{2,6},{6,10},{10,14},{3,7},{... | collective-permute-start | bytes 3145736 | tf_op jit(solution)/shard_map/while/body/eval_jaxpr/ppermute | solution.py:17
  525.2 4.8 slice-start.4
  527.1 3.0 slice-start.5
  540.2 3.8 copy-start
  544.0 3.2 copy-start.5
  547.2 2.2 copy-start.2
  547.2 2.6 slice-start
  548.5 2.4 slice-start.1
  548.8 24.7 %slice-start.2 = ((s8[8388608]{0:T(1024)(128)(4,1)}), s8[4194304]{0:T(1024)(128)(4,1)S(1)}, s32[]{:S(2)}) async-start(s8[8388608]{0:T(1024)(128)(4,1)} %bitcast.138), calls=%async_computation.9 | async-start | bytes 8388608 | tf_op jit(solution)/shard_map/while
  550.9 22.6 %slice-start.3 = ((s8[8388608]{0:T(1024)(128)(4,1)}), s8[4194304]{0:T(1024)(128)(4,1)S(1)}, s32[]{:S(2)}) async-start(s8[8388608]{0:T(1024)(128)(4,1)} %bitcast.138), calls=%async_computation.10 | async-start | bytes 8388608 | tf_op jit(solution)/shard_map/while
  573.5 5.7 copy-start.1
  579.8 24.1 %collective-permute-start = (bf16[512,1024]{1,0:T(8,128)(2,1)S(1)}, bf16[512,1024]{1,0:T(8,128)(2,1)S(1)}, u32[]{:S(2)}, u32[]{:S(2)}) collective-permute-start(bf16[512,1024]{1,0:T(8,128)(2,1)S(1)} %get-tuple-element.564), channel_id=1, source_target_pairs={{0,4},{4,8},{8,12},{1,5},{5,9},{9,13},{2,6},{6,10},{10,14},{3,7},{... | collective-permute-start | bytes 3145736 | tf_op jit(solution)/shard_map/while/body/eval_jaxpr/ppermute | solution.py:17
  605.9 9.3 %all-to-all-start = ((bf16[4,2,128]{2,1,0:T(2,128)(2,1)}), bf16[4,2,128]{2,1,0:T(2,128)(2,1)S(1)}, u32[]{:S(2)}, u32[]{:S(2)}) async-start(bf16[4,2,128]{2,1,0:T(2,128)(2,1)} %reshape.179), calls=%async_computation | async-start | bytes 4096 | tf_op jit(solution)/shard_map/all_to_all | solution.py:169
  628.6 23.7 %copy-start.3 = (bf16[2,64]{1,0:T(2,128)(2,1)}, bf16[2,64]{1,0:T(2,128)(2,1)S(1)}, u32[]{:S(2)}) copy-start(bf16[2,64]{1,0:T(2,128)(2,1)S(1)} %get-tuple-element.459) | copy-start | bytes 772
  628.6 23.7 %copy-start.4 = (bf16[2,64]{1,0:T(2,128)(2,1)}, bf16[2,64]{1,0:T(2,128)(2,1)S(1)}, u32[]{:S(2)}) copy-start(bf16[2,64]{1,0:T(2,128)(2,1)S(1)} %get-tuple-element.460) | copy-start | bytes 772
  629.2 9.6 %all-to-all-start.1 = ((bf16[8,2,64]{2,1,0:T(2,128)(2,1)}), bf16[8,2,64]{2,1,0:T(2,128)(2,1)S(1)}, u32[]{:S(2)}, u32[]{:S(2)}) async-start(bf16[8,2,64]{2,1,0:T(2,128)(2,1)} %broadcast_in_dim.139), calls=%async_computation.1 | async-start | bytes 8192 | tf_op jit(solution)/shard_map/all_to_all | solution.py:32
  639.5 12.0 %all-to-all-start.2 = ((f32[16,2,16]{2,1,0:T(2,128)}), f32[16,2,16]{2,1,0:T(2,128)S(1)}, u32[]{:S(2)}, u32[]{:S(2)}) async-start(f32[16,2,16]{2,1,0:T(2,128)} %broadcast_in_dim.140), calls=%async_computation.2 | async-start | bytes 32768 | tf_op jit(solution)/shard_map/all_to_all | solution.py:32
Sparse Core Ops, SparseCore 0:
  9.6 33.4 all-gather.7
  44.8 69.1 all-gather.5
  115.7 83.7 all-gather.9
  201.0 84.0 all-gather.11
where the time goes:
time: 659 us
  waiting for transfers between devices  376 us (57%)
  matrix products  173 us (26%)
  starting transfers between devices  29.6 us (4%)
  local copies, waits for them, and re-layouts  26.4 us (4%)
  other arithmetic  22.3 us (3%)
  between operations  14.6 us (2%)
  blocking collectives  13.3 us (2%)
    dot_general x4, matrix products, encode_layer(): upward = jnp.dot(mixed, w_up, preferred_element_type=jnp.float32)  90.3 us
    all_gather x1, waiting for transfers between devices, per_device(): lax.all_gather(w_down, 'tensor', axis=1, tiled=True)  85.6 us
    all_gather x1, waiting for transfers between devices, per_device(): lax.all_gather(w_up, 'tensor', axis=2, tiled=True)  85.5 us
    ppermute x4, waiting for transfers between devices, from_behind(): lax.ppermute(value, axis, [(source, source + steps) for source in range(i...  80.8 us
    all_gather x1, waiting for transfers between devices, per_device(): lax.all_gather(w_qkv, 'tensor', axis=3, tiled=True)  70.9 us
    all_gather x1, waiting for transfers between devices, per_device(): lax.all_gather(w_out, 'tensor', axis=1, tiled=True)  32.4 us
    dot_general x8, matrix products, local_reduce(): jnp.einsum('sgk,gkd->gsd', left_parts, right_parts, preferred_element_typ...  24.7 us
    ppermute x4, starting transfers between devices, from_behind(): lax.ppermute(value, axis, [(source, source + steps) for source in range(i...  16.8 us
  transfers between devices with their start and end apart: 11, of which 11 were waited for; matrix products, arithmetic and copies ran while one was open for 0% of the time, Pallas kernels for 0%

commit v1 on v0

--- a/solution.py
+++ b/solution.py
@@ -9,6 +9,19 @@
 SOFTMAX_TEMPER = 0.05
 EPSILON = 1e-06
 LAYER_EPSILON = 1e-12
+
+
+def ring_gather(x, axis, dim):
+    ways = lax.axis_size(axis)
+    up = [(d, (d + 1) % ways) for d in range(ways)]
+    down = [(d, (d - 1) % ways) for d in range(ways)]
+    earlier, later = ([x], [x])
+    for _ in range(ways // 2):
+        earlier.append(lax.ppermute(earlier[-1], axis, up))
+    for _ in range((ways - 1) // 2):
+        later.append(lax.ppermute(later[-1], axis, down))
+    line = jnp.concatenate([*earlier[::-1], *later[1:]], axis=dim)
+    return jnp.roll(line, (lax.axis_index(axis) - ways // 2) * x.shape[dim], axis=dim)
 
 
 def from_behind(value, axis, steps):
@@ -121,7 +134,7 @@
         lax.all_gather(w_qkv, "tensor", axis=3, tiled=True),
         lax.all_gather(w_out, "tensor", axis=1, tiled=True),
         lax.all_gather(w_up, "tensor", axis=2, tiled=True),
-        lax.all_gather(w_down, "tensor", axis=1, tiled=True),
+        ring_gather(w_down, "tensor", 1),
     )
     share = seq_count // tensor_count
     first_seq = lax.axis_index("tensor") * share

time: 659 us -> 631 us (0.958)
  waiting for transfers between devices: 376 us -> 313 us
  local copies, waits for them, and re-layouts: 26.4 us -> 56.1 us
    ppermute x0 -> x3, waiting for transfers between devices: none -> 151 us  [the longest x2 151 us: ring_gather(): earlier.append(lax.ppermute(earlier[-1], axis, up))]
    all_gather x1 -> x0, waiting for transfers between devices: 85.6 us -> none  [per_device(): lax.all_gather(w_down, 'tensor', axis=1, tiled=True)]
    all_gather x1, waiting for transfers between devices: 70.9 us -> 0.01 us  [per_device(): lax.all_gather(w_qkv, 'tensor', axis=3, tiled=True)]
    all_gather x1, waiting for transfers between devices: 32.4 us -> 0.01 us  [per_device(): lax.all_gather(w_out, 'tensor', axis=1, tiled=True)]
    all_gather x1, waiting for transfers between devices: 85.5 us -> 61.1 us  [per_device(): lax.all_gather(w_up, 'tensor', axis=2, tiled=True)]
    unnamed x9 -> x22, local copies, waits for them, and re-layouts: 0.76 us -> 19.3 us
    dynamic_slice x0 -> x1, local copies, waits for them, and re-layouts: none -> 7.86 us  [ring_gather(): jnp.roll(line, (lax.axis_index(axis) - ways // 2) * x.shape[dim], axis=dim)]
  transfers between devices with their start and end apart: 11 -> 13, of which waited for: 11 -> 10; matrix products, arithmetic and copies ran while one was open for 0% -> 5% of each run, Pallas kernels for 0% -> 0%
where the time goes in v1:
time: 631 us
  waiting for transfers between devices  313 us (50%)
  matrix products  173 us (27%)
  local copies, waits for them, and re-layouts  56.1 us (9%)
  starting transfers between devices  35 us (6%)
  other arithmetic  22 us (3%)
  between operations  14.6 us (2%)
  blocking collectives  13.3 us (2%)
    ppermute x2, waiting for transfers between devices, ring_gather(): earlier.append(lax.ppermute(earlier[-1], axis, up))  151 us
    dot_general x4, matrix products, encode_layer(): upward = jnp.dot(mixed, w_up, preferred_element_type=jnp.float32)  90.3 us
    ppermute x4, waiting for transfers between devices, from_behind(): lax.ppermute(value, axis, [(source, source + steps) for source in range(i...  81 us
    all_gather x1, waiting for transfers between devices, per_device(): lax.all_gather(w_up, 'tensor', axis=2, tiled=True)  61.1 us
    dot_general x8, matrix products, local_reduce(): jnp.einsum('sgk,gkd->gsd', left_parts, right_parts, preferred_element_typ...  24.7 us
    unnamed x22, local copies, waits for them, and re-layouts  19.3 us
    ppermute x4, starting transfers between devices, from_behind(): lax.ppermute(value, axis, [(source, source + steps) for source in range(i...  16.8 us
    dot_general x4, matrix products, encode_layer(): jnp.einsum('qhe,khe->hqk', query_heads, key_heads, preferred_element_type...  15.1 us
  transfers between devices with their start and end apart: 13, of which 10 were waited for; matrix products, arithmetic and copies ran while one was open for 5% of the time, Pallas kernels for 0%

profile of v1, /device:TPU:0, one launch (start us, length us, event | category | flops | bytes accessed | tf_op | source)
XLA Modules:
  0.0 630.6 jit_solution(7756604383222901046)
XLA Ops:
  9.4 2.1 collective-permute-start.1
  11.5 66.2 %collective-permute-done.1 = bf16[1,1024,1024]{2,1,0:T(8,128)(2,1)} collective-permute-done((bf16[1,1024,1024]{2,1,0:T(8,128)(2,1)}, bf16[1,1024,1024]{2,1,0:T(8,128)(2,1)}, u32[]{:S(2)}, u32[]{:S(2)}) %collective-permute-start.1) | collective-permute-done | bytes 2097184 | tf_op jit(solution)/shard_map/ppermute | solution.py:20
  78.5 2.5 collective-permute-start.3
  81.8 84.6 %collective-permute-done.2 = bf16[1,1024,1024]{2,1,0:T(8,128)(2,1)} collective-permute-done((bf16[1,1024,1024]{2,1,0:T(8,128)(2,1)}, bf16[1,1024,1024]{2,1,0:T(8,128)(2,1)}, u32[]{:S(2)}, u32[]{:S(2)}) %collective-permute-start.2) | collective-permute-done | bytes 2097184 | tf_op jit(solution)/shard_map/ppermute | solution.py:20
  166.4 3.1 constant_dynamic-update-slice_fusion.7
  169.5 3.1 constant_dynamic-update-slice_fusion.6
  174.1 3.1 constant_dynamic-update-slice_fusion.4
  177.2 3.1 constant_dynamic-update-slice_fusion.3
  180.3 3.1 constant_dynamic-update-slice_fusion.2
  184.9 3.3 constant_dynamic-update-slice_fusion
  188.2 7.9 %constant_dynamic-slice_fusion.1 = bf16[1,4096,1024]{2,1,0:T(8,128)(2,1)} fusion(bf16[1,8192,1024]{2,1,0:T(8,128)(2,1)} %constant_dynamic-update-slice_fusion, s32[]{:T(128)S(6)} %select_n.125), kind=kLoop, calls=%fused_computation.83 | loop fusion | bytes 16777220 | tf_op jit(solution)/shard_map/jit(_roll_dynamic)/dynamic_slice | solution.py:24
  196.1 61.1 %all-gather.9.cloned.1.call-done = bf16[1,1024,4096]{2,1,0:T(8,128)(2,1)} async-done(((bf16[1,1024,1024]{2,1,0:T(8,128)(2,1)}), bf16[1,1024,4096]{2,1,0:T(8,128)(2,1)}) %all-gather.9.cloned.1.call-update) | async-done | bytes 8388624 | tf_op jit(solution)/shard_map/all_gather | solution.py:136
  257.3 318.3 %while.18 = (s32[]{:T(128)}, bf16[512,1024]{1,0:T(8,128)(2,1)S(1)}, f32[1,1024]{1,0:T(1,128)S(1)}, pred[]{:T(512)}, s32[]{:T(128)}, /*index=5*/bf16[2,512,1024]{...) while((s32[]{:T(128)}, bf16[512,1024]{1,0:T(8,128)(2,1)S(1)}, ...), condition=%wide.region_9.10_spmd.clone, body=%wide.region_0.9_spmd.clone.sunk | while | flops 14147382272 | bytes 201464576 | solution.py:177
  257.5 1.8 bitcast_select_fusion.2
  259.4 3.0 multiply_convert_fusion.6
  262.4 2.3 fusion.92
  264.7 2.3 fusion.91
  270.2 2.3 copy.78
  272.5 3.8 fusion.93
  276.3 3.1 fusion.94
  283.1 22.6 %fusion.96 = bf16[512,4096]{1,0:T(8,128)(2,1)S(1)} fusion(bf16[512,1024]{1,0:T(8,128)(2,1)S(1)} %multiply_convert_fusion.7, bf16[1,1024,4096]{2,1,0:T(8,128)(2,1)S(1)} %bitcast.140), kind=kOutput, calls=%fused_computation.7.clone.1 | convolution fusion | flops 4431282176 | bytes 13631488 | tf_op jit(solution)/shard_map/while/body/eval_jaxpr/dot_general | solution.py:99
  305.7 4.9 convert_reduce_fusion.6
  312.0 3.4 collective-permute-start
  316.0 21.5 %collective-permute-done = bf16[512,1024]{1,0:T(8,128)(2,1)S(1)} collective-permute-done((bf16[512,1024]{1,0:T(8,128)(2,1)S(1)}, bf16[512,1024]{1,0:T(8,128)(2,1)S(1)}, u32[]{:S(2)}, u32[]{:S(2)}) %collective-permute-start) | collective-permute-done | bytes 1048608 | tf_op jit(solution)/shard_map/while/body/eval_jaxpr/ppermute | solution.py:30
  337.6 1.8 bitcast_select_fusion.2
  339.4 3.0 multiply_convert_fusion.6
  342.4 2.3 fusion.92
  344.8 2.3 fusion.91
  350.2 2.3 copy.78
  352.5 3.8 fusion.93
  356.3 3.1 fusion.94
  363.2 22.6 %fusion.96 = bf16[512,4096]{1,0:T(8,128)(2,1)S(1)} fusion(bf16[512,1024]{1,0:T(8,128)(2,1)S(1)} %multiply_convert_fusion.7, bf16[1,1024,4096]{2,1,0:T(8,128)(2,1)S(1)} %bitcast.140), kind=kOutput, calls=%fused_computation.7.clone.1 | convolution fusion | flops 4431282176 | bytes 13631488 | tf_op jit(solution)/shard_map/while/body/eval_jaxpr/dot_general | solution.py:99
  385.8 4.9 convert_reduce_fusion.6
  392.0 4.5 collective-permute-start
  397.1 20.7 %collective-permute-done = bf16[512,1024]{1,0:T(8,128)(2,1)S(1)} collective-permute-done((bf16[512,1024]{1,0:T(8,128)(2,1)S(1)}, bf16[512,1024]{1,0:T(8,128)(2,1)S(1)}, u32[]{:S(2)}, u32[]{:S(2)}) %collective-permute-start) | collective-permute-done | bytes 1048608 | tf_op jit(solution)/shard_map/while/body/eval_jaxpr/ppermute | solution.py:30
  417.8 1.8 bitcast_select_fusion.2
  419.6 3.0 multiply_convert_fusion.6
  422.7 2.3 fusion.92
  425.0 2.3 fusion.91
  430.4 2.3 copy.78
  432.7 3.8 fusion.93
  436.5 3.1 fusion.94
  443.4 22.6 %fusion.96 = bf16[512,4096]{1,0:T(8,128)(2,1)S(1)} fusion(bf16[512,1024]{1,0:T(8,128)(2,1)S(1)} %multiply_convert_fusion.7, bf16[1,1024,4096]{2,1,0:T(8,128)(2,1)S(1)} %bitcast.140), kind=kOutput, calls=%fused_computation.7.clone.1 | convolution fusion | flops 4431282176 | bytes 13631488 | tf_op jit(solution)/shard_map/while/body/eval_jaxpr/dot_general | solution.py:99
  466.0 4.9 convert_reduce_fusion.6
  472.2 4.5 collective-permute-start
  477.3 19.8 %collective-permute-done = bf16[512,1024]{1,0:T(8,128)(2,1)S(1)} collective-permute-done((bf16[512,1024]{1,0:T(8,128)(2,1)S(1)}, bf16[512,1024]{1,0:T(8,128)(2,1)S(1)}, u32[]{:S(2)}, u32[]{:S(2)}) %collective-permute-start) | collective-permute-done | bytes 1048608 | tf_op jit(solution)/shard_map/while/body/eval_jaxpr/ppermute | solution.py:30
  497.1 1.8 bitcast_select_fusion.2
  499.0 3.0 multiply_convert_fusion.6
  502.0 2.3 fusion.92
  504.3 2.3 fusion.91
  509.8 2.3 copy.78
  512.1 3.8 fusion.93
  515.9 3.1 fusion.94
  522.8 22.6 %fusion.96 = bf16[512,4096]{1,0:T(8,128)(2,1)S(1)} fusion(bf16[512,1024]{1,0:T(8,128)(2,1)S(1)} %multiply_convert_fusion.7, bf16[1,1024,4096]{2,1,0:T(8,128)(2,1)S(1)} %bitcast.140), kind=kOutput, calls=%fused_computation.7.clone.1 | convolution fusion | flops 4431282176 | bytes 13631488 | tf_op jit(solution)/shard_map/while/body/eval_jaxpr/dot_general | solution.py:99
  545.4 4.9 convert_reduce_fusion.6
  551.6 4.5 collective-permute-start
  556.7 19.0 %collective-permute-done = bf16[512,1024]{1,0:T(8,128)(2,1)S(1)} collective-permute-done((bf16[512,1024]{1,0:T(8,128)(2,1)S(1)}, bf16[512,1024]{1,0:T(8,128)(2,1)S(1)}, u32[]{:S(2)}, u32[]{:S(2)}) %collective-permute-start) | collective-permute-done | bytes 1048608 | tf_op jit(solution)/shard_map/while/body/eval_jaxpr/ppermute | solution.py:30
  577.7 4.0 all-to-all-start
  581.7 5.3 all-to-all-done
  587.1 13.3 %all-gather = bf16[16,1,4,1,64]{4,2,3,1,0:T(4,128)(2,1)S(1)} all-gather(bf16[4,1,4,1,64]{4,2,3,1,0:T(4,128)(2,1)S(1)} %bitcast_bitcast_fusion), channel_id=2, replica_groups=mesh['dp'=8,'pipe'=4,'tensor'=4] {'pipe'}, dimensions={0}, use_global_device_ids=true | all-gather | bytes 10240 | tf_op jit(solution)/shard_map/all_gather | solution.py:34
  601.1 4.3 all-to-all-start.1
  605.4 5.3 all-to-all-done.1
  611.4 4.4 all-to-all-start.2
  615.8 7.6 %all-to-all-done.2 = f32[16,2,16]{2,1,0:T(2,128)S(1)} async-done(((f32[16,2,16]{2,1,0:T(2,128)}), f32[16,2,16]{2,1,0:T(2,128)S(1)}, u32[]{:S(2)}, u32[]{:S(2)}) %all-to-all-start.2) | async-done | bytes 2080 | tf_op jit(solution)/shard_map/all_to_all | solution.py:45
  (189 shorter events, 43.3 us)
Async XLA Ops:
  7.2 165.4 %copy-start.1 = (bf16[1,1024,1024]{2,1,0:T(8,128)(2,1)S(1)}, bf16[1,1024,1024]{2,1,0:T(8,128)(2,1)}, u32[]{:S(2)}) copy-start(bf16[1,1024,1024]{2,1,0:T(8,128)(2,1)} %param.21) | copy-start | bytes 6291460
  7.2 188.9 %all-gather.7.cloned.1.call-start = ((), (), s32[]{:S(2)}) async-start(), calls=%async_computation.4 | async-start | bytes 2621440 | tf_op jit(solution)/shard_map/all_gather | solution.py:135
  7.9 188.2 %all-gather.5.cloned.1.call-start = ((), (), s32[]{:S(2)}) async-start(), calls=%async_computation.3 | async-start | bytes 7864320 | tf_op jit(solution)/shard_map/all_gather | solution.py:134
  8.7 248.5 %all-gather.9.cloned.1.call-start = ((), (), s32[]{:S(2)}) async-start(), calls=%async_computation.5 | async-start | bytes 10485760 | tf_op jit(solution)/shard_map/all_gather | solution.py:136
  9.4 68.3 %collective-permute-start.1 = (bf16[1,1024,1024]{2,1,0:T(8,128)(2,1)}, bf16[1,1024,1024]{2,1,0:T(8,128)(2,1)}, u32[]{:S(2)}, u32[]{:S(2)}) collective-permute-start(bf16[1,1024,1024]{2,1,0:T(8,128)(2,1)} %param.21), channel_id=1, source_target_pairs={{0,1},{1,2},{2,3},{3,0},{4,5},{5,6},{6,7},{7,4},{8,9},{9,10},{10,1... | collective-permute-start | bytes 6291464 | tf_op jit(solution)/shard_map/ppermute | solution.py:20
  77.7 88.8 %collective-permute-start.2 = (bf16[1,1024,1024]{2,1,0:T(8,128)(2,1)}, bf16[1,1024,1024]{2,1,0:T(8,128)(2,1)}, u32[]{:S(2)}, u32[]{:S(2)}) collective-permute-start(bf16[1,1024,1024]{2,1,0:T(8,128)(2,1)} %collective-permute-done.1), channel_id=1, source_target_pairs={{0,1},{1,2},{2,3},{3,0},{4,5},{5,6},{6,7},{7,4},{8,9},{9,10},{10,1... | collective-permute-start | bytes 6291464 | tf_op jit(solution)/shard_map/ppermute | solution.py:20
  78.5 95.6 %collective-permute-start.3 = (bf16[1,1024,1024]{2,1,0:T(8,128)(2,1)}, bf16[1,1024,1024]{2,1,0:T(8,128)(2,1)}, u32[]{:S(2)}, u32[]{:S(2)}) collective-permute-start(bf16[1,1024,1024]{2,1,0:T(8,128)(2,1)} %param.21), channel_id=1, source_target_pairs={{0,3},{1,0},{2,1},{3,2},{4,7},{5,4},{6,5},{7,6},{8,11},{9,8},{10,9... | collective-permute-start | bytes 6291464 | tf_op jit(solution)/shard_map/ppermute | solution.py:22
  188.2 69.1 %copy-start.2 = (f32[1,1024]{1,0:T(1,128)S(1)}, f32[1,1024]{1,0:T(1,128)}, u32[]{:S(2)}) copy-start(f32[1,1024]{1,0:T(1,128)} %param.23) | copy-start | bytes 12292
  188.2 69.1 %copy-start.3 = (f32[1,1024]{1,0:T(1,128)S(1)}, f32[1,1024]{1,0:T(1,128)}, u32[]{:S(2)}) copy-start(f32[1,1024]{1,0:T(1,128)} %param.22) | copy-start | bytes 12292
  257.3 358.5 %copy-start.7 = (s32[1,2]{1,0:T(1,128)S(1)}, s32[1,2]{1,0:T(1,128)}, u32[]{:S(2)}) copy-start(s32[1,2]{1,0:T(1,128)} %param.17) | copy-start | bytes 28
  257.5 4.9 slice-start.4
  259.4 3.0 slice-start.5
  272.5 3.8 copy-start
  276.3 3.2 copy-start.6
  279.4 2.6 slice-start.2
  280.7 2.4 slice-start.3
  281.1 24.7 %slice-start = ((s8[8388608]{0:T(1024)(128)(4,1)}), s8[4194304]{0:T(1024)(128)(4,1)S(1)}, s32[]{:S(2)}) async-start(s8[8388608]{0:T(1024)(128)(4,1)} %bitcast.130), calls=%async_computation.6 | async-start | bytes 8388608 | tf_op jit(solution)/shard_map/while
  283.1 22.6 %slice-start.1 = ((s8[8388608]{0:T(1024)(128)(4,1)}), s8[4194304]{0:T(1024)(128)(4,1)S(1)}, s32[]{:S(2)}) async-start(s8[8388608]{0:T(1024)(128)(4,1)} %bitcast.130), calls=%async_computation.7 | async-start | bytes 8388608 | tf_op jit(solution)/shard_map/while
  312.0 25.6 %collective-permute-start = (bf16[512,1024]{1,0:T(8,128)(2,1)S(1)}, bf16[512,1024]{1,0:T(8,128)(2,1)S(1)}, u32[]{:S(2)}, u32[]{:S(2)}) collective-permute-start(bf16[512,1024]{1,0:T(8,128)(2,1)S(1)} %get-tuple-element.564), channel_id=1, source_target_pairs={{0,4},{4,8},{8,12},{1,5},{5,9},{9,13},{2,6},{6,10},{10,14},{3,7},{... | collective-permute-start | bytes 3145736 | tf_op jit(solution)/shard_map/while/body/eval_jaxpr/ppermute | solution.py:30
  337.6 4.8 slice-start.4
  339.4 3.0 slice-start.5
  352.5 3.8 copy-start
  356.3 3.2 copy-start.6
  359.5 2.6 slice-start.2
  360.8 2.4 slice-start.3
  361.1 24.7 %slice-start = ((s8[8388608]{0:T(1024)(128)(4,1)}), s8[4194304]{0:T(1024)(128)(4,1)S(1)}, s32[]{:S(2)}) async-start(s8[8388608]{0:T(1024)(128)(4,1)} %bitcast.130), calls=%async_computation.6 | async-start | bytes 8388608 | tf_op jit(solution)/shard_map/while
  363.2 22.6 %slice-start.1 = ((s8[8388608]{0:T(1024)(128)(4,1)}), s8[4194304]{0:T(1024)(128)(4,1)S(1)}, s32[]{:S(2)}) async-start(s8[8388608]{0:T(1024)(128)(4,1)} %bitcast.130), calls=%async_computation.7 | async-start | bytes 8388608 | tf_op jit(solution)/shard_map/while
  392.0 25.8 %collective-permute-start = (bf16[512,1024]{1,0:T(8,128)(2,1)S(1)}, bf16[512,1024]{1,0:T(8,128)(2,1)S(1)}, u32[]{:S(2)}, u32[]{:S(2)}) collective-permute-start(bf16[512,1024]{1,0:T(8,128)(2,1)S(1)} %get-tuple-element.564), channel_id=1, source_target_pairs={{0,4},{4,8},{8,12},{1,5},{5,9},{9,13},{2,6},{6,10},{10,14},{3,7},{... | collective-permute-start | bytes 3145736 | tf_op jit(solution)/shard_map/while/body/eval_jaxpr/ppermute | solution.py:30
  417.8 4.8 slice-start.4
  419.6 3.0 slice-start.5
  432.7 3.8 copy-start
  436.5 3.2 copy-start.6
  439.7 2.6 slice-start.2
  441.0 2.4 slice-start.3
  441.3 24.7 %slice-start = ((s8[8388608]{0:T(1024)(128)(4,1)}), s8[4194304]{0:T(1024)(128)(4,1)S(1)}, s32[]{:S(2)}) async-start(s8[8388608]{0:T(1024)(128)(4,1)} %bitcast.130), calls=%async_computation.6 | async-start | bytes 8388608 | tf_op jit(solution)/shard_map/while
  443.4 22.6 %slice-start.1 = ((s8[8388608]{0:T(1024)(128)(4,1)}), s8[4194304]{0:T(1024)(128)(4,1)S(1)}, s32[]{:S(2)}) async-start(s8[8388608]{0:T(1024)(128)(4,1)} %bitcast.130), calls=%async_computation.7 | async-start | bytes 8388608 | tf_op jit(solution)/shard_map/while
  472.2 24.9 %collective-permute-start = (bf16[512,1024]{1,0:T(8,128)(2,1)S(1)}, bf16[512,1024]{1,0:T(8,128)(2,1)S(1)}, u32[]{:S(2)}, u32[]{:S(2)}) collective-permute-start(bf16[512,1024]{1,0:T(8,128)(2,1)S(1)} %get-tuple-element.564), channel_id=1, source_target_pairs={{0,4},{4,8},{8,12},{1,5},{5,9},{9,13},{2,6},{6,10},{10,14},{3,7},{... | collective-permute-start | bytes 3145736 | tf_op jit(solution)/shard_map/while/body/eval_jaxpr/ppermute | solution.py:30
  497.1 4.8 slice-start.4
  499.0 3.0 slice-start.5
  512.1 3.8 copy-start
  515.9 3.2 copy-start.6
  519.0 2.6 slice-start.2
  520.3 2.4 slice-start.3
  520.7 24.7 %slice-start = ((s8[8388608]{0:T(1024)(128)(4,1)}), s8[4194304]{0:T(1024)(128)(4,1)S(1)}, s32[]{:S(2)}) async-start(s8[8388608]{0:T(1024)(128)(4,1)} %bitcast.130), calls=%async_computation.6 | async-start | bytes 8388608 | tf_op jit(solution)/shard_map/while
  522.7 22.6 %slice-start.1 = ((s8[8388608]{0:T(1024)(128)(4,1)}), s8[4194304]{0:T(1024)(128)(4,1)S(1)}, s32[]{:S(2)}) async-start(s8[8388608]{0:T(1024)(128)(4,1)} %bitcast.130), calls=%async_computation.7 | async-start | bytes 8388608 | tf_op jit(solution)/shard_map/while
  551.6 24.0 %collective-permute-start = (bf16[512,1024]{1,0:T(8,128)(2,1)S(1)}, bf16[512,1024]{1,0:T(8,128)(2,1)S(1)}, u32[]{:S(2)}, u32[]{:S(2)}) collective-permute-start(bf16[512,1024]{1,0:T(8,128)(2,1)S(1)} %get-tuple-element.564), channel_id=1, source_target_pairs={{0,4},{4,8},{8,12},{1,5},{5,9},{9,13},{2,6},{6,10},{10,14},{3,7},{... | collective-permute-start | bytes 3145736 | tf_op jit(solution)/shard_map/while/body/eval_jaxpr/ppermute | solution.py:30
  577.7 9.3 %all-to-all-start = ((bf16[4,2,128]{2,1,0:T(2,128)(2,1)}), bf16[4,2,128]{2,1,0:T(2,128)(2,1)S(1)}, u32[]{:S(2)}, u32[]{:S(2)}) async-start(bf16[4,2,128]{2,1,0:T(2,128)(2,1)} %reshape.179), calls=%async_computation | async-start | bytes 4096 | tf_op jit(solution)/shard_map/all_to_all | solution.py:182
  600.5 23.6 %copy-start.4 = (bf16[2,64]{1,0:T(2,128)(2,1)}, bf16[2,64]{1,0:T(2,128)(2,1)S(1)}, u32[]{:S(2)}) copy-start(bf16[2,64]{1,0:T(2,128)(2,1)S(1)} %get-tuple-element.459) | copy-start | bytes 772
  600.5 23.6 %copy-start.5 = (bf16[2,64]{1,0:T(2,128)(2,1)}, bf16[2,64]{1,0:T(2,128)(2,1)S(1)}, u32[]{:S(2)}) copy-start(bf16[2,64]{1,0:T(2,128)(2,1)S(1)} %get-tuple-element.460) | copy-start | bytes 772
  601.1 9.6 %all-to-all-start.1 = ((bf16[8,2,64]{2,1,0:T(2,128)(2,1)}), bf16[8,2,64]{2,1,0:T(2,128)(2,1)S(1)}, u32[]{:S(2)}, u32[]{:S(2)}) async-start(bf16[8,2,64]{2,1,0:T(2,128)(2,1)} %broadcast_in_dim.139), calls=%async_computation.1 | async-start | bytes 8192 | tf_op jit(solution)/shard_map/all_to_all | solution.py:45
  611.4 12.0 %all-to-all-start.2 = ((f32[16,2,16]{2,1,0:T(2,128)}), f32[16,2,16]{2,1,0:T(2,128)S(1)}, u32[]{:S(2)}, u32[]{:S(2)}) async-start(f32[16,2,16]{2,1,0:T(2,128)} %broadcast_in_dim.140), calls=%async_computation.2 | async-start | bytes 32768 | tf_op jit(solution)/shard_map/all_to_all | solution.py:45
Sparse Core Ops, SparseCore 0:
  9.6 50.4 all-gather.6
  61.8 110.2 all-gather.4
  173.7 83.3 all-gather.8
